TPU v7x, 32 devices: a whole 2x2x4 slice. The times are simulated.
32 devices in a mesh: rowa: 2 (over x), rowb: 4 (over z), col: 4 (over y, core).
Axes of the slice: x: 2, y: 2, z: 4, core: 2. Of those that a mesh axis runs over, the one named last changes fastest.
Arguments:
- table: float32 [65536, 512], P(('rowa', 'rowb'), 'col'), may hold values from -12 to 12
- start: float32 [16, 512], P(None, 'col'), may hold values from -6 to 6
Outputs:
- right_vectors: float32 [16, 512], P(None, 'col')
- left_images: float32 [16, 65536], P(None, ('rowa', 'rowb'))
- strengths: float32 [16], replicated
All inputs are finite; a program needn't handle non-finite values.
Results may differ from a plain program's by a relative error of at most 0.00014.
Values sent between devices are 32-bit elements.
A program may use at most 64 MiB of HBM per device.

v0:
```python
import jax
import jax.numpy as jnp
from jax import lax
from jax.sharding import PartitionSpec as P

STEPS = 8
high = lax.Precision.HIGHEST


def apply_rows(vectors, table):
    return lax.dot_general(
        vectors, table, (((1,), (1,)), ((), ())), precision=high, preferred_element_type=jnp.float32
    )


def outer_gram(products):
    return lax.dot_general(
        products,
        products,
        (((1,), (1,)), ((), ())),
        precision=high,
        preferred_element_type=jnp.float32,
    )


def normalize(gram, products):
    lower = jnp.linalg.cholesky(gram)
    return (jax.scipy.linalg.solve_triangular(lower, products, lower=True), lower)


def own_columns(vectors, start):
    width = start.shape[1]
    offset = lax.axis_index("col") * width
    return lax.dynamic_slice_in_dim(vectors, offset, width, 1)


def on_device(table, start):
    regrouped = lax.all_to_all(table, "col", split_axis=0, concat_axis=1, tiled=True)
    rows_total = table.shape[0] * lax.axis_size("rowa") * lax.axis_size("rowb")
    vectors = lax.all_gather(start, "col", axis=1, tiled=True)
    partial_cover = lax.dot_general(
        regrouped,
        regrouped,
        (((0,), (0,)), ((), ())),
        precision=high,
        preferred_element_type=jnp.float32,
    )
    cover = lax.psum(partial_cover, ("rowa", "rowb", "col"))
    previous = vectors
    lower = None
    for step in range(STEPS):
        previous = vectors
        products = jnp.dot(vectors, cover, precision=high, preferred_element_type=jnp.float32)
        vectors, lower = normalize(outer_gram(products), products)
    images = apply_rows(previous, regrouped)
    left = lax.all_gather(images, "col", axis=1, tiled=True)
    return (own_columns(vectors, start), left, jnp.diagonal(lower) / rows_total)


def solution(mesh):
    placed = (P(("rowa", "rowb"), "col"), P(None, "col"))
    return jax.shard_map(
        on_device,
        mesh=mesh,
        in_specs=placed,
        out_specs=(P(None, "col"), P(None, ("rowa", "rowb")), P()),
        check_vma=False,
    )
```

profile of v0, /device:TPU:0, one launch (start us, length us, event | category | flops | bytes accessed | tf_op | source)
XLA Modules:
  0.0 275.0 jit_solution(15089997109972043354)
XLA Ops:
  7.2 54.6 %all_to_all.19 = f32[4,2048,128]{2,1,0:T(8,128)} all-to-all(f32[4,2048,128]{2,1,0:T(8,128)} %bitcast.126), channel_id=1, replica_groups=mesh['rowa'=2,'rowb'=4,'col'=4] {'col'}, dimensions={0} | all-to-all | bytes 8388608 | tf_op jit(solution)/shard_map/all_to_all | solution.py:38
  61.8 5.4 %copy.21 = f32[2048,4,128]{0,2,1:T(8,128)} copy(f32[2048,4,128]{2,0,1:T(8,128)} %bitcast.125) | data formatting | bytes 8388608 | tf_op jit(solution)/shard_map/all_to_all | solution.py:38
  67.1 10.3 %fusion.48 = f32[512,512]{1,0:T(8,128)} fusion(f32[2048,512]{0,1:T(8,128)} %bitcast.123), kind=kOutput, calls=%fused_computation.78 | convolution fusion | flops 6442450944 | bytes 5242880 | tf_op jit(solution)/shard_map/dot_general | solution.py:41
  77.5 5.4 %all_gather.6 = f32[16,512]{1,0:T(8,128)S(1)} all-gather(f32[16,128]{1,0:T(8,128)S(1)} %copy-done.1), channel_id=1, replica_groups=mesh['rowa'=2,'rowb'=4,'col'=4] {'col'}, dimensions={1}, use_global_device_ids=true | all-gather | bytes 40960 | tf_op jit(solution)/shard_map/all_gather | solution.py:40
  82.9 126.5 %all-reduce.2.cloned.1.call-done = f32[512,512]{1,0:T(8,128)} async-done(((f32[512,512]{1,0:T(8,128)}), f32[512,512]{1,0:T(8,128)}) %all-reduce.2.cloned.1.call-update) | async-done | bytes 1048592 | tf_op jit(solution)/shard_map/psum | solution.py:48
  209.4 2.0 fusion.49
  211.3 0.1 fusion.50
  211.6 1.5 cholesky.134
  213.1 0.6 compare_reduce_fusion.7
  213.7 0.6 fusion.2
  214.4 1.2 custom-call.14
  215.6 0.2 fusion
  215.8 1.9 fusion.51
  217.9 1.5 cholesky.145
  219.4 0.6 compare_reduce_fusion.6
  220.1 0.6 fusion.3
  220.7 1.2 custom-call.15
  222.0 0.2 fusion.27
  222.2 1.9 fusion.53
  224.3 1.5 cholesky.156
  225.8 0.6 compare_reduce_fusion.5
  226.4 0.6 fusion.4
  227.1 1.2 custom-call.16
  228.3 0.2 fusion.24
  228.6 0.6 fusion.55
  229.2 0.1 fusion.56
  229.4 1.5 cholesky.167
  230.9 0.6 compare_reduce_fusion.4
  231.6 0.6 fusion.5
  232.2 1.2 custom-call.17
  233.5 0.2 fusion.21
  233.7 0.6 fusion.57
  234.3 0.1 fusion.58
  234.6 1.5 cholesky.178
  236.1 0.6 compare_reduce_fusion.3
  236.7 0.6 fusion.6
  237.4 1.2 custom-call.18
  238.6 0.2 fusion.18
  238.8 0.6 fusion.59
  239.5 0.1 fusion.60
  239.7 1.5 cholesky.189
  241.2 0.6 compare_reduce_fusion.2
  241.8 0.6 fusion.7
  242.5 1.2 custom-call.19
  243.7 0.2 fusion.15
  244.0 0.6 fusion.61
  244.6 0.1 fusion.62
  244.8 1.5 cholesky.200
  246.3 0.6 compare_reduce_fusion.1
  247.0 0.6 fusion.8
  247.6 1.2 custom-call.20
  248.9 0.2 fusion.12
  249.1 4.3 %fusion.65 = f32[16,2048]{1,0:T(8,128)S(1)} fusion(f32[16,512]{1,0:T(8,128)S(1)} %fusion.12, f32[2048,512]{0,1:T(8,128)} %bitcast.124), kind=kOutput, calls=%fused_computation.95 | convolution fusion | flops 201326592 | bytes 4358144 | tf_op jit(solution)/shard_map/dot_general | solution.py:11
  253.4 7.1 %all_gather.7 = f32[16,8192]{1,0:T(8,128)S(1)} all-gather(f32[16,2048]{1,0:T(8,128)S(1)} %fusion.65), channel_id=1, replica_groups=mesh['rowa'=2,'rowb'=4,'col'=4] {'col'}, dimensions={1}, use_global_device_ids=true | all-gather | bytes 655360 | tf_op jit(solution)/shard_map/all_gather | solution.py:56
  260.5 0.6 fusion.63
  261.3 1.5 cholesky.211
  262.8 0.6 compare_reduce_fusion
  263.5 0.6 select_bitcast_fusion
  264.1 1.2 custom-call.21
  265.4 0.2 fusion.9
  265.6 0.7 gather_fusion
  266.3 0.5 broadcast_multiply_fusion
  266.8 0.6 constant_dynamic-slice_fusion
  267.4 0.8 copy.32
  (34 shorter events, 1.5 us)
Async XLA Ops:
  7.2 202.2 %all-reduce.2.cloned.1.call-start = ((), (), s32[]{:S(2)}) async-start(), calls=%async_computation.1 | async-start | bytes 2097152 | tf_op jit(solution)/shard_map/psum | solution.py:48
  67.1 10.4 %copy-start.1 = (f32[16,128]{1,0:T(8,128)S(1)}, f32[16,128]{1,0:T(8,128)}, u32[]{:S(2)}) copy-start(f32[16,128]{1,0:T(8,128)} %param.6) | copy-start | bytes 24580
  209.4 19.2 %copy-start = (f32[512,512]{1,0:T(8,128)S(1)}, f32[512,512]{1,0:T(8,128)}, u32[]{:S(2)}) copy-start(f32[512,512]{1,0:T(8,128)} %all-reduce.2.cloned.1.call-done) | copy-start | bytes 3145732
Sparse Core Ops, SparseCore 0:
  77.6 131.7 all-reduce.1
where the time goes:
time: 276 us; the launch traced here: 275 us
  waiting for transfers between devices  127 us (46%)
  blocking collectives  67 us (24%)
  other arithmetic  32.8 us (12%)
  matrix products  26.4 us (10%)
  between operations  14.2 us (5%)
  local copies, waits for them, and re-layouts  8.11 us (3%)
    psum x1, waiting for transfers between devices, on_device(): cover = lax.psum(partial_cover, ('rowa', 'rowb', 'col'))  126 us
    all_to_all x1, blocking collectives, on_device(): lax.all_to_all(table, 'col', split_axis=0, concat_axis=1, tiled=True)  54.6 us
    another operation x24, other arithmetic, normalize(): lower = jnp.linalg.cholesky(gram)  17.2 us
    another operation x16, other arithmetic, normalize(): jax.scipy.linalg.solve_triangular(lower, products, lower=True)  15 us
    dot_general x1, matrix products, on_device(): lax.dot_general(regrouped, regrouped, (((0,), (0,)), ((), ())), precision...  10.3 us
    dot_general x8, matrix products, on_device(): jnp.dot(vectors, cover, precision=high, preferred_element_type=jnp.float32)  8.81 us
    all_gather x1, blocking collectives, on_device(): left = lax.all_gather(images, 'col', axis=1, tiled=True)  7.1 us
  transfers between devices with their start and end apart: 1, of which 1 were waited for; matrix products, arithmetic and copies ran while one was open for 0% of the time, Pallas kernels for 0%

commit v1 on v0

--- a/solution.py
+++ b/solution.py
@@ -45,7 +45,7 @@
         precision=high,
         preferred_element_type=jnp.float32,
     )
-    cover = lax.psum(partial_cover, ("rowa", "rowb", "col"))
+    cover = jnp.sum(lax.all_gather(partial_cover, ("rowa", "rowb", "col")), axis=0)
     previous = vectors
     lower = None
     for step in range(STEPS):

time: 276 us -> 348 us (1.26)
  waiting for transfers between devices: 127 us -> 190 us
  other arithmetic: 32.8 us -> 45.1 us
  matrix products: 26.4 us -> 22.6 us
    all_gather x0 -> x1, waiting for transfers between devices: none -> 190 us  [on_device(): lax.all_gather(partial_cover, ('rowa', 'rowb', 'col'))]
    psum x1 -> x0, waiting for transfers between devices: 126 us -> none  [on_device(): cover = lax.psum(partial_cover, ('rowa', 'rowb', 'col'))]
    reduce_sum x0 -> x1, other arithmetic: none -> 12.3 us  [on_device(): jnp.sum(lax.all_gather(partial_cover, ('rowa', 'rowb', 'col')), axis=0)]
    dot_general x8, matrix products: 8.81 us -> 5.07 us  [on_device(): jnp.dot(vectors, cover, precision=high, preferred_element_type=jnp.float32)]
where the time goes in v1:
time: 348 us; the launch traced here: 347 us
  waiting for transfers between devices  190 us (55%)
  blocking collectives  67.1 us (19%)
  other arithmetic  45.1 us (13%)
  matrix products  22.6 us (6%)
  between operations  14.2 us (4%)
  local copies, waits for them, and re-layouts  8.11 us (2%)
    all_gather x1, waiting for transfers between devices, on_device(): lax.all_gather(partial_cover, ('rowa', 'rowb', 'col'))  190 us
    all_to_all x1, blocking collectives, on_device(): lax.all_to_all(table, 'col', split_axis=0, concat_axis=1, tiled=True)  54.5 us
    another operation x24, other arithmetic, normalize(): lower = jnp.linalg.cholesky(gram)  17.2 us
    another operation x16, other arithmetic, normalize(): jax.scipy.linalg.solve_triangular(lower, products, lower=True)  15 us
    reduce_sum x1, other arithmetic, on_device(): jnp.sum(lax.all_gather(partial_cover, ('rowa', 'rowb', 'col')), axis=0)  12.3 us
    dot_general x1, matrix products, on_device(): lax.dot_general(regrouped, regrouped, (((0,), (0,)), ((), ())), precision...  10.3 us
    all_gather x1, blocking collectives, on_device(): left = lax.all_gather(images, 'col', axis=1, tiled=True)  7.17 us
  transfers between devices with their start and end apart: 1, of which 1 were waited for; matrix products, arithmetic and copies ran while one was open for 0% of the time, Pallas kernels for 0%

profile of v1, /device:TPU:0, one launch (start us, length us, event | category | flops | bytes accessed | tf_op | source)
XLA Modules:
  0.0 347.1 jit_solution(489775004383667283)
XLA Ops:
  7.2 54.5 %all_to_all.19 = f32[4,2048,128]{2,1,0:T(8,128)} all-to-all(f32[4,2048,128]{2,1,0:T(8,128)} %bitcast.128), channel_id=1, replica_groups=mesh['rowa'=2,'rowb'=4,'col'=4] {'col'}, dimensions={0} | all-to-all | bytes 8388608 | tf_op jit(solution)/shard_map/all_to_all | solution.py:38
  61.8 5.4 %copy.21 = f32[2048,4,128]{0,2,1:T(8,128)} copy(f32[2048,4,128]{2,0,1:T(8,128)} %bitcast.127) | data formatting | bytes 8388608 | tf_op jit(solution)/shard_map/all_to_all | solution.py:38
  67.1 10.3 %fusion.48 = f32[512,512]{1,0:T(8,128)} fusion(f32[2048,512]{0,1:T(8,128)} %bitcast.124), kind=kOutput, calls=%fused_computation.78 | convolution fusion | flops 6442450944 | bytes 5242880 | tf_op jit(solution)/shard_map/dot_general | solution.py:41
  77.5 5.4 %all_gather.14 = f32[16,512]{1,0:T(8,128)S(1)} all-gather(f32[16,128]{1,0:T(8,128)S(1)} %copy-done), channel_id=1, replica_groups=mesh['rowa'=2,'rowb'=4,'col'=4] {'col'}, dimensions={1}, use_global_device_ids=true | all-gather | bytes 40960 | tf_op jit(solution)/shard_map/all_gather | solution.py:40
  82.8 190.0 %all-gather.3.cloned.1.call-done = f32[16384,512]{1,0:T(8,128)} async-done(((f32[512,512]{1,0:T(8,128)}), f32[16384,512]{1,0:T(8,128)}) %all-gather.3.cloned.1.call-update) | async-done | bytes 33554448 | tf_op jit(solution)/shard_map/all_gather | solution.py:48
  272.8 12.3 %reduce_sum.9 = f32[512,512]{1,0:T(8,128)S(1)} reduce(f32[32,512,512]{2,1,0:T(8,128)} %bitcast.126, f32[]{:T(128)} %constant.45.clone.1), dimensions={0}, to_apply=%region_0.0 | reduce | flops 8126464 | bytes 34603012 | tf_op jit(solution)/shard_map/reduce_sum | solution.py:48
  285.1 0.7 fusion.49
  286.0 1.5 cholesky.134
  287.5 0.6 compare_reduce_fusion.7
  288.1 0.6 fusion.2
  288.8 1.2 custom-call.14
  290.0 0.2 fusion
  290.3 0.6 fusion.51
  290.9 0.1 fusion.52
  291.1 1.5 cholesky.145
  292.6 0.6 compare_reduce_fusion.6
  293.3 0.6 fusion.3
  293.9 1.2 custom-call.15
  295.2 0.2 fusion.27
  295.4 0.6 fusion.53
  296.0 0.1 fusion.54
  296.3 1.5 cholesky.156
  297.8 0.6 compare_reduce_fusion.5
  298.4 0.6 fusion.4
  299.1 1.2 custom-call.16
  300.3 0.2 fusion.24
  300.5 0.6 fusion.55
  301.2 0.1 fusion.56
  301.4 1.5 cholesky.167
  302.9 0.6 compare_reduce_fusion.4
  303.5 0.6 fusion.5
  304.2 1.2 custom-call.17
  305.4 0.2 fusion.21
  305.7 0.6 fusion.57
  306.5 1.5 cholesky.178
  308.0 0.6 compare_reduce_fusion.3
  308.7 0.6 fusion.6
  309.3 1.2 custom-call.18
  310.6 0.2 fusion.18
  310.8 0.6 fusion.59
  311.7 1.5 cholesky.189
  313.2 0.6 compare_reduce_fusion.2
  313.8 0.6 fusion.7
  314.5 1.2 custom-call.19
  315.7 0.2 fusion.15
  315.9 0.6 fusion.61
  316.6 0.1 fusion.62
  316.8 1.5 cholesky.200
  318.3 0.6 compare_reduce_fusion.1
  318.9 0.6 fusion.8
  319.6 1.2 custom-call.20
  320.8 0.2 fusion.12
  321.1 4.3 %fusion.65 = f32[16,2048]{1,0:T(8,128)S(1)} fusion(f32[16,512]{1,0:T(8,128)S(1)} %fusion.12, f32[2048,512]{0,1:T(8,128)} %bitcast.125), kind=kOutput, calls=%fused_computation.95 | convolution fusion | flops 201326592 | bytes 4358144 | tf_op jit(solution)/shard_map/dot_general | solution.py:11
  325.4 0.6 fusion.63
  326.0 7.2 %all_gather.15 = f32[16,8192]{1,0:T(8,128)S(1)} all-gather(f32[16,2048]{1,0:T(8,128)S(1)} %fusion.65), channel_id=1, replica_groups=mesh['rowa'=2,'rowb'=4,'col'=4] {'col'}, dimensions={1}, use_global_device_ids=true | all-gather | bytes 655360 | tf_op jit(solution)/shard_map/all_gather | solution.py:56
  333.4 1.5 cholesky.211
  334.9 0.6 compare_reduce_fusion
  335.5 0.6 select_bitcast_fusion
  336.2 1.2 custom-call.21
  337.4 0.2 fusion.9
  337.6 0.7 gather_fusion
  338.3 0.5 broadcast_multiply_fusion
  338.8 0.6 constant_dynamic-slice_fusion
  339.4 0.8 copy.31
  (33 shorter events, 1.6 us)
Async XLA Ops:
  7.2 265.7 %all-gather.3.cloned.1.call-start = ((), (), s32[]{:S(2)}) async-start(), calls=%async_computation.1 | async-start | bytes 34603008 | tf_op jit(solution)/shard_map/all_gather | solution.py:48
  67.1 10.3 %copy-start = (f32[16,128]{1,0:T(8,128)S(1)}, f32[16,128]{1,0:T(8,128)}, u32[]{:S(2)}) copy-start(f32[16,128]{1,0:T(8,128)} %param.6) | copy-start | bytes 24580
Sparse Core Ops, SparseCore 0:
  77.6 195.2 all-gather.2
